TPU v7x, 32 devices: a whole 2x2x4 slice. The times are simulated.
32 devices in a mesh: mol: 2 (over x), pts: 16 (over z, y, core).
Axes of the slice: x: 2, y: 2, z: 4, core: 2. Of those that a mesh axis runs over, the one named last changes fastest.
Arguments:
- points_map: bfloat16 [12800, 800], P(('mol', 'pts')), parts along dimension 0, may hold values from -0.21875 to 0.21875
- trial: bfloat16 [12800, 128], P('mol'), parts along dimension 0, may hold values from -6 to 6
- core: bfloat16 [12800, 6400], P(('mol', 'pts')), parts along dimension 0, may hold values from -2 to 4, as said below
- walkers: bfloat16 [1600, 12, 128], P('mol'), parts along dimension 0, may hold values from -6 to 6
- draws: int32 [12800, 12], P(('mol', 'pts')), parts along dimension 0, may hold values from 0 to 3
Outputs:
- new_walkers: bfloat16 [1600, 12, 128], P(('mol', 'pts')), parts along dimension 0
- energy: float32 [24], P('mol'), parts along dimension 0
There are 2 independent parts, one for each index of `mol`. A program takes and returns all parts, laid end to end along the dimension named above; each array names one. Nothing has to cross between parts.
Inputs may be any that keep to these rules, and one draw needn't show every extreme that they name: core is symmetric.
All inputs are finite; a program needn't handle non-finite values.
Results may differ from a plain program's by a relative error of at most 0.018.
Values may be sent and summed in bfloat16 or wider, within the bound.
A program may use at most 192 MiB of HBM per device.

v0:
```python
import math
import jax
import jax.numpy as jnp
from jax import lax
from jax.sharding import PartitionSpec as P

TAYLOR = 3
GAUSS_NODES = (-2.3344142, -0.7419637, 0.7419637, 2.3344142)
FIELD_STEP = 0.15


def node_lookup(draws):
    values = jnp.zeros(draws.shape, jnp.float32)
    for number, node in enumerate(GAUSS_NODES):
        values = values + jnp.where(draws == number, node, 0.0).astype(jnp.float32)
    return values


def body(points_map, trial, core, walkers, draws):
    point_rows = points_map.shape[0]
    orbitals = points_map.shape[1]
    walker_count = walkers.shape[1]
    occupied = walkers.shape[2]
    point_first = lax.axis_index("pts") * point_rows
    trial_here = lax.dynamic_slice_in_dim(trial, point_first, point_rows, 0)
    flat_walkers = walkers.reshape(orbitals, walker_count * occupied)
    orbit = (
        jnp.dot(points_map, flat_walkers, preferred_element_type=jnp.float32)
        .astype(jnp.bfloat16)
        .reshape(point_rows, walker_count, occupied)
    )
    density = (
        jnp.sum(orbit.astype(jnp.float32) * trial_here.astype(jnp.float32)[:, None, :], axis=2)
        / math.sqrt(occupied)
    ).astype(jnp.bfloat16)
    core_block = core
    potential = jnp.dot(
        core_block,
        lax.all_gather(density, "pts", axis=0, tiled=True),
        preferred_element_type=jnp.float32,
    )
    field = FIELD_STEP * (node_lookup(draws) - FIELD_STEP * potential)
    local_walkers = jnp.moveaxis(orbit, 1, 0)
    core_block = core.astype(jnp.float32)

    def per_walker(operands):
        left_orb, right_orb = operands
        forward = jnp.dot(left_orb, trial.T, preferred_element_type=jnp.float32)
        backward = jnp.dot(trial_here, right_orb.T, preferred_element_type=jnp.float32)
        return jnp.sum(core_block * forward * backward)

    exchange = (
        lax.map(
            per_walker,
            (local_walkers, jnp.moveaxis(lax.all_gather(orbit, "pts", axis=0, tiled=True), 1, 0)),
        )
        / occupied
    )
    hartree = jnp.sum(density.astype(jnp.float32) * potential, axis=0)
    total_points = point_rows * lax.axis_size("pts")
    energy = lax.psum((hartree - exchange) / (2.0 * total_points), "pts")
    own_rows = orbitals // lax.axis_size("pts")
    map_full = lax.all_gather(points_map, "pts", axis=0, tiled=True)
    field_full = lax.all_gather(field, "pts", axis=0, tiled=True)
    own_cols = walker_count * occupied // lax.axis_size("pts")
    col_start = lax.axis_index("pts") * own_cols
    cols_walkers = lax.dynamic_slice_in_dim(flat_walkers, col_start, own_cols, 1)
    walker_ids = (col_start + jnp.arange(own_cols, dtype=jnp.int32)) // occupied
    field_cols = jnp.take(field_full, walker_ids, axis=1)
    running_cols = cols_walkers.astype(jnp.float32)
    term_cols = cols_walkers
    for degree in range(1, TAYLOR + 1):
        current_cols = jnp.dot(map_full, term_cols, preferred_element_type=jnp.float32).astype(
            jnp.bfloat16
        )
        scaled_cols = (field_cols * current_cols.astype(jnp.float32)).astype(jnp.bfloat16)
        summed_cols = jnp.einsum(
            "pi,pc->ic", map_full, scaled_cols, preferred_element_type=jnp.float32
        )
        term_cols = (summed_cols / degree).astype(jnp.bfloat16)
        running_cols = running_cols + term_cols.astype(jnp.float32)
    placed = lax.all_to_all(
        running_cols.astype(jnp.bfloat16), "pts", split_axis=0, concat_axis=1, tiled=True
    )
    return (placed.reshape(own_rows, walker_count, occupied), energy)


def solution(mesh):
    placed = (
        P(("mol", "pts"), None),
        P("mol", None),
        P(("mol", "pts"), None),
        P("mol", None, None),
        P(("mol", "pts"), None),
    )
    return jax.shard_map(
        body,
        mesh=mesh,
        in_specs=placed,
        out_specs=(P(("mol", "pts"), None, None), P("mol")),
        check_vma=False,
    )
```

profile of v0, /device:TPU:0, one launch (start us, length us, event | category | flops | bytes accessed | tf_op | source)
XLA Modules:
  0.0 381.3 jit_solution(17466998609298275406)
XLA Ops:
  20.1 25.9 %all-gather = bf16[16,400,12]{1,2,0:T(8,128)(2,1)S(1)} all-gather(bf16[1,400,12]{1,2,0:T(8,128)(2,1)S(1)} %fusion.25), channel_id=1, replica_groups=mesh['mol'=2,'pts'=16] {'pts'}, dimensions={0}, use_global_device_ids=true | all-gather | bytes 163200 | tf_op jit(solution)/shard_map/all_gather | solution.py:39
  50.4 21.2 %all-gather.1 = f32[16,400,12]{1,2,0:T(8,128)S(1)} all-gather(f32[1,400,12]{1,2,0:T(8,128)S(1)} %get-tuple-element.75), channel_id=1, replica_groups=mesh['mol'=2,'pts'=16] {'pts'}, dimensions={0}, use_global_device_ids=true | all-gather | bytes 326400 | tf_op jit(solution)/shard_map/all_gather | solution.py:64
  73.6 36.2 %all-gather.5.cloned.1.call-done = bf16[6400,800]{1,0:T(8,128)(2,1)} async-done(((bf16[400,800]{1,0:T(8,128)(2,1)}), bf16[6400,800]{1,0:T(8,128)(2,1)}) %all-gather.5.cloned.1.call-update) | async-done | bytes 10240016 | tf_op jit(solution)/shard_map/all_gather | solution.py:63
  109.8 13.0 %convolution_convert_fusion.4 = bf16[96,800]{1,0:T(8,128)(2,1)S(1)} fusion(bf16[6400,800]{1,0:T(8,128)(2,1)} %all-gather.5.cloned.1.call-done, f32[96,6400]{1,0:T(8,128)S(1)} %gather_fusion, pred[96]{0:T(512)(128)(4,1)S(1)} %compare_and_fusion, bf16[800,1536]{0,1:T(8,128)(2,1)} %bitcast.74, s32[]{:T(128)S(6)} %select_n.54), kind=kOutput, calls=%fused_computation.28 | convolution fusion | flops 1969228800 | bytes 25720932 | tf_op jit(solution)/shard_map/pi,pc->ic/dot_general | solution.py:77
  122.9 13.4 %fusion.17 = bf16[96,800]{1,0:T(8,128)(2,1)S(1)} fusion(bf16[6400,800]{1,0:T(8,128)(2,1)} %all-gather.5.cloned.1.call-done, bf16[96,800]{1,0:T(8,128)(2,1)S(1)} %convolution_convert_fusion.4, f32[96,6400]{1,0:T(8,128)S(1)} %gather_fusion, pred[96]{0:T(512)(128)(4,1)S(1)} %compare_and_fusion), kind=kOutput, calls=%fused_computation.29 | convolution fusion | flops 1969305600 | bytes 13004896 | tf_op jit(solution)/shard_map/pi,pc->ic/dot_general | solution.py:77
  136.2 13.6 %fusion.22 = bf16[800,96]{0,1:T(8,128)(2,1)S(1)} fusion(bf16[6400,800]{1,0:T(8,128)(2,1)} %all-gather.5.cloned.1.call-done, bf16[96,800]{1,0:T(8,128)(2,1)S(1)} %fusion.17, f32[96,6400]{1,0:T(8,128)S(1)} %gather_fusion, pred[96]{0:T(512)(128)(4,1)S(1)} %compare_and_fusion, bf16[96,800]{1,0:T(8,128)(2,1)S(1)} %convolution_convert_fusion.4, ...), kind=kOutput, calls=%fused_computation.34 | convolution fusion | flops 1969920000 | bytes 26237444 | tf_op jit(solution)/shard_map/pi,pc->ic/dot_general | solution.py:77
  150.8 4.7 %all-to-all-start = ((bf16[16,50,96]{2,1,0:T(8,128)(2,1)}), bf16[16,50,96]{2,1,0:T(8,128)(2,1)S(1)}, u32[]{:S(2)}, u32[]{:S(2)}) async-start(bf16[16,50,96]{2,1,0:T(8,128)(2,1)} %all_to_all.12), calls=%async_computation | async-start | bytes 458752 | tf_op jit(solution)/shard_map/all_to_all | solution.py:82
  155.5 7.2 %convert_element_type.121 = f32[400,6400]{1,0:T(8,128)} convert(bf16[400,6400]{1,0:T(8,128)(2,1)} %param.9) | non-fusion elementwise | flops 2560000 | bytes 15360000 | tf_op jit(solution)/shard_map/convert_element_type | solution.py:44
  164.0 5.1 %all-to-all-done = bf16[16,50,96]{2,1,0:T(8,128)(2,1)S(1)} async-done(((bf16[16,50,96]{2,1,0:T(8,128)(2,1)}), bf16[16,50,96]{2,1,0:T(8,128)(2,1)S(1)}, u32[]{:S(2)}, u32[]{:S(2)}) %all-to-all-start) | async-done | bytes 153632 | tf_op jit(solution)/shard_map/all_to_all | solution.py:82
  169.3 48.3 %all-gather.7.cloned.1.call-done = bf16[6400,12,128]{2,0,1:T(8,128)(2,1)} async-done(((bf16[400,12,128]{2,0,1:T(8,128)(2,1)}), bf16[6400,12,128]{2,0,1:T(8,128)(2,1)}) %all-gather.7.cloned.1.call-update) | async-done | bytes 19660816 | tf_op jit(solution)/shard_map/all_gather | solution.py:55
  217.6 123.1 %while.10 = (s32[]{:T(128)}, f32[12]{0:T(128)S(1)}, bf16[12,400,128]{2,1,0:T(8,128)(2,1)}, bf16[6400,128]{1,0:T(8,128)(2,1)}, f32[400,6400]{1,0:T(8,128)}, /*ind...) while((s32[]{:T(128)}, f32[12]{0:T(128)S(1)}, bf16[12,400,128]{2,1,0:T(8,128)(2,1)}, ...), condition=%wide.region_4.5_spmd, body=%wide.region_2.4_spmd.sunk | while | flops 1318400000 | bytes 75162760 | solution.py:53
  222.0 5.1 %fusion.57 = f32[]{:T(128)} fusion(f32[400,6400]{1,0:T(8,128)S(1)} %convolution_bitcast_fusion.3, f32[400,6400]{1,0:T(8,128)S(1)} %copy-done, bf16[6400,128]{1,0:T(8,128)(2,1)} %get-tuple-element.138, bf16[12,400,128]{2,1,0:T(8,128)(2,1)} %get-tuple-element.137, s32[]{:T(128)} %get-tuple-element.127), kind=kOutput, calls=%fused_computation.4.clone.1 | convolution fusion | flops 663040000 | bytes 22221316 | tf_op jit(solution)/shard_map/while/body/eval_jaxpr/dot_general | solution.py:48
  232.3 5.1 %fusion.57 = f32[]{:T(128)} fusion(f32[400,6400]{1,0:T(8,128)S(1)} %convolution_bitcast_fusion.3, f32[400,6400]{1,0:T(8,128)S(1)} %copy-done, bf16[6400,128]{1,0:T(8,128)(2,1)} %get-tuple-element.138, bf16[12,400,128]{2,1,0:T(8,128)(2,1)} %get-tuple-element.137, s32[]{:T(128)} %get-tuple-element.127), kind=kOutput, calls=%fused_computation.4.clone.1 | convolution fusion | flops 663040000 | bytes 22221316 | tf_op jit(solution)/shard_map/while/body/eval_jaxpr/dot_general | solution.py:48
  242.5 5.1 %fusion.57 = f32[]{:T(128)} fusion(f32[400,6400]{1,0:T(8,128)S(1)} %convolution_bitcast_fusion.3, f32[400,6400]{1,0:T(8,128)S(1)} %copy-done, bf16[6400,128]{1,0:T(8,128)(2,1)} %get-tuple-element.138, bf16[12,400,128]{2,1,0:T(8,128)(2,1)} %get-tuple-element.137, s32[]{:T(128)} %get-tuple-element.127), kind=kOutput, calls=%fused_computation.4.clone.1 | convolution fusion | flops 663040000 | bytes 22221316 | tf_op jit(solution)/shard_map/while/body/eval_jaxpr/dot_general | solution.py:48
  252.8 5.1 %fusion.57 = f32[]{:T(128)} fusion(f32[400,6400]{1,0:T(8,128)S(1)} %convolution_bitcast_fusion.3, f32[400,6400]{1,0:T(8,128)S(1)} %copy-done, bf16[6400,128]{1,0:T(8,128)(2,1)} %get-tuple-element.138, bf16[12,400,128]{2,1,0:T(8,128)(2,1)} %get-tuple-element.137, s32[]{:T(128)} %get-tuple-element.127), kind=kOutput, calls=%fused_computation.4.clone.1 | convolution fusion | flops 663040000 | bytes 22221316 | tf_op jit(solution)/shard_map/while/body/eval_jaxpr/dot_general | solution.py:48
  263.0 5.1 %fusion.57 = f32[]{:T(128)} fusion(f32[400,6400]{1,0:T(8,128)S(1)} %convolution_bitcast_fusion.3, f32[400,6400]{1,0:T(8,128)S(1)} %copy-done, bf16[6400,128]{1,0:T(8,128)(2,1)} %get-tuple-element.138, bf16[12,400,128]{2,1,0:T(8,128)(2,1)} %get-tuple-element.137, s32[]{:T(128)} %get-tuple-element.127), kind=kOutput, calls=%fused_computation.4.clone.1 | convolution fusion | flops 663040000 | bytes 22221316 | tf_op jit(solution)/shard_map/while/body/eval_jaxpr/dot_general | solution.py:48
  273.3 5.1 %fusion.57 = f32[]{:T(128)} fusion(f32[400,6400]{1,0:T(8,128)S(1)} %convolution_bitcast_fusion.3, f32[400,6400]{1,0:T(8,128)S(1)} %copy-done, bf16[6400,128]{1,0:T(8,128)(2,1)} %get-tuple-element.138, bf16[12,400,128]{2,1,0:T(8,128)(2,1)} %get-tuple-element.137, s32[]{:T(128)} %get-tuple-element.127), kind=kOutput, calls=%fused_computation.4.clone.1 | convolution fusion | flops 663040000 | bytes 22221316 | tf_op jit(solution)/shard_map/while/body/eval_jaxpr/dot_general | solution.py:48
  283.5 5.1 %fusion.57 = f32[]{:T(128)} fusion(f32[400,6400]{1,0:T(8,128)S(1)} %convolution_bitcast_fusion.3, f32[400,6400]{1,0:T(8,128)S(1)} %copy-done, bf16[6400,128]{1,0:T(8,128)(2,1)} %get-tuple-element.138, bf16[12,400,128]{2,1,0:T(8,128)(2,1)} %get-tuple-element.137, s32[]{:T(128)} %get-tuple-element.127), kind=kOutput, calls=%fused_computation.4.clone.1 | convolution fusion | flops 663040000 | bytes 22221316 | tf_op jit(solution)/shard_map/while/body/eval_jaxpr/dot_general | solution.py:48
  293.8 5.1 %fusion.57 = f32[]{:T(128)} fusion(f32[400,6400]{1,0:T(8,128)S(1)} %convolution_bitcast_fusion.3, f32[400,6400]{1,0:T(8,128)S(1)} %copy-done, bf16[6400,128]{1,0:T(8,128)(2,1)} %get-tuple-element.138, bf16[12,400,128]{2,1,0:T(8,128)(2,1)} %get-tuple-element.137, s32[]{:T(128)} %get-tuple-element.127), kind=kOutput, calls=%fused_computation.4.clone.1 | convolution fusion | flops 663040000 | bytes 22221316 | tf_op jit(solution)/shard_map/while/body/eval_jaxpr/dot_general | solution.py:48
  304.1 5.1 %fusion.57 = f32[]{:T(128)} fusion(f32[400,6400]{1,0:T(8,128)S(1)} %convolution_bitcast_fusion.3, f32[400,6400]{1,0:T(8,128)S(1)} %copy-done, bf16[6400,128]{1,0:T(8,128)(2,1)} %get-tuple-element.138, bf16[12,400,128]{2,1,0:T(8,128)(2,1)} %get-tuple-element.137, s32[]{:T(128)} %get-tuple-element.127), kind=kOutput, calls=%fused_computation.4.clone.1 | convolution fusion | flops 663040000 | bytes 22221316 | tf_op jit(solution)/shard_map/while/body/eval_jaxpr/dot_general | solution.py:48
  314.3 5.1 %fusion.57 = f32[]{:T(128)} fusion(f32[400,6400]{1,0:T(8,128)S(1)} %convolution_bitcast_fusion.3, f32[400,6400]{1,0:T(8,128)S(1)} %copy-done, bf16[6400,128]{1,0:T(8,128)(2,1)} %get-tuple-element.138, bf16[12,400,128]{2,1,0:T(8,128)(2,1)} %get-tuple-element.137, s32[]{:T(128)} %get-tuple-element.127), kind=kOutput, calls=%fused_computation.4.clone.1 | convolution fusion | flops 663040000 | bytes 22221316 | tf_op jit(solution)/shard_map/while/body/eval_jaxpr/dot_general | solution.py:48
  324.6 5.1 %fusion.57 = f32[]{:T(128)} fusion(f32[400,6400]{1,0:T(8,128)S(1)} %convolution_bitcast_fusion.3, f32[400,6400]{1,0:T(8,128)S(1)} %copy-done, bf16[6400,128]{1,0:T(8,128)(2,1)} %get-tuple-element.138, bf16[12,400,128]{2,1,0:T(8,128)(2,1)} %get-tuple-element.137, s32[]{:T(128)} %get-tuple-element.127), kind=kOutput, calls=%fused_computation.4.clone.1 | convolution fusion | flops 663040000 | bytes 22221316 | tf_op jit(solution)/shard_map/while/body/eval_jaxpr/dot_general | solution.py:48
  334.8 5.1 %fusion.57 = f32[]{:T(128)} fusion(f32[400,6400]{1,0:T(8,128)S(1)} %convolution_bitcast_fusion.3, f32[400,6400]{1,0:T(8,128)S(1)} %copy-done, bf16[6400,128]{1,0:T(8,128)(2,1)} %get-tuple-element.138, bf16[12,400,128]{2,1,0:T(8,128)(2,1)} %get-tuple-element.137, s32[]{:T(128)} %get-tuple-element.127), kind=kOutput, calls=%fused_computation.4.clone.1 | convolution fusion | flops 663040000 | bytes 22221316 | tf_op jit(solution)/shard_map/while/body/eval_jaxpr/dot_general | solution.py:48
  341.4 33.1 %psum.7 = f32[12]{0:T(128)} all-reduce(f32[12]{0:T(128)S(1)} %subtract_multiply_fusion), channel_id=1, replica_groups=mesh['mol'=2,'pts'=16] {'pts'}, use_global_device_ids=true, to_apply=%region_5.6 | all-reduce | flops 12 | bytes 96 | tf_op jit(solution)/shard_map/psum | solution.py:61
  (85 shorter events, 84.3 us)
Async XLA Ops:
  7.2 102.7 %all-gather.5.cloned.1.call-start = ((), (), s32[]{:S(2)}) async-start(), calls=%async_computation.1 | async-start | bytes 12185600 | tf_op jit(solution)/shard_map/all_gather | solution.py:63
  7.9 4.6 %copy-start.3 = (bf16[400,800]{1,0:T(8,128)(2,1)S(1)}, bf16[400,800]{1,0:T(8,128)(2,1)}, u32[]{:S(2)}) copy-start(bf16[400,800]{1,0:T(8,128)(2,1)} %param.7) | copy-start | bytes 1920004
  7.9 209.7 %all-gather.7.cloned.1.call-start = ((), (), s32[]{:S(2)}) async-start(), calls=%async_computation.2 | async-start | bytes 20889600 | tf_op jit(solution)/shard_map/all_gather | solution.py:55
  17.9 32.5 %copy-start.1 = (bf16[400,12,128]{2,1,0:T(8,128)(2,1)}, bf16[400,12,128]{2,1,0:T(8,128)(2,1)S(1)}, u32[]{:S(2)}) copy-start(bf16[400,12,128]{2,1,0:T(8,128)(2,1)S(1)} %reshape.85) | copy-start | bytes 3686404
  17.9 28.4 %copy-start.4 = (s32[400,12]{0,1:T(8,128)S(1)}, s32[400,12]{0,1:T(8,128)}, u32[]{:S(2)}) copy-start(s32[400,12]{0,1:T(8,128)} %param.11) | copy-start | bytes 57604
  150.8 18.3 %all-to-all-start = ((bf16[16,50,96]{2,1,0:T(8,128)(2,1)}), bf16[16,50,96]{2,1,0:T(8,128)(2,1)S(1)}, u32[]{:S(2)}, u32[]{:S(2)}) async-start(bf16[16,50,96]{2,1,0:T(8,128)(2,1)} %all_to_all.12), calls=%async_computation | async-start | bytes 458752 | tf_op jit(solution)/shard_map/all_to_all | solution.py:82
  155.5 7.2 %copy-start.2 = (bf16[400,12,128]{2,1,0:T(8,128)(2,1)S(1)}, bf16[400,12,128]{2,1,0:T(8,128)(2,1)}, u32[]{:S(2)}) copy-start(bf16[400,12,128]{2,1,0:T(8,128)(2,1)} %copy-done.1) | copy-start | bytes 3686404
  217.6 4.4 %copy-start = (f32[400,6400]{1,0:T(8,128)S(1)}, f32[400,6400]{1,0:T(8,128)}, u32[]{:S(2)}) copy-start(f32[400,6400]{1,0:T(8,128)} %get-tuple-element.139) | copy-start | bytes 30720004 | tf_op jit(solution)/shard_map/while
  227.9 4.4 %copy-start = (f32[400,6400]{1,0:T(8,128)S(1)}, f32[400,6400]{1,0:T(8,128)}, u32[]{:S(2)}) copy-start(f32[400,6400]{1,0:T(8,128)} %get-tuple-element.139) | copy-start | bytes 30720004 | tf_op jit(solution)/shard_map/while
  238.1 4.4 %copy-start = (f32[400,6400]{1,0:T(8,128)S(1)}, f32[400,6400]{1,0:T(8,128)}, u32[]{:S(2)}) copy-start(f32[400,6400]{1,0:T(8,128)} %get-tuple-element.139) | copy-start | bytes 30720004 | tf_op jit(solution)/shard_map/while
  248.4 4.4 %copy-start = (f32[400,6400]{1,0:T(8,128)S(1)}, f32[400,6400]{1,0:T(8,128)}, u32[]{:S(2)}) copy-start(f32[400,6400]{1,0:T(8,128)} %get-tuple-element.139) | copy-start | bytes 30720004 | tf_op jit(solution)/shard_map/while
  258.6 4.4 %copy-start = (f32[400,6400]{1,0:T(8,128)S(1)}, f32[400,6400]{1,0:T(8,128)}, u32[]{:S(2)}) copy-start(f32[400,6400]{1,0:T(8,128)} %get-tuple-element.139) | copy-start | bytes 30720004 | tf_op jit(solution)/shard_map/while
  268.9 4.4 %copy-start = (f32[400,6400]{1,0:T(8,128)S(1)}, f32[400,6400]{1,0:T(8,128)}, u32[]{:S(2)}) copy-start(f32[400,6400]{1,0:T(8,128)} %get-tuple-element.139) | copy-start | bytes 30720004 | tf_op jit(solution)/shard_map/while
  279.1 4.4 %copy-start = (f32[400,6400]{1,0:T(8,128)S(1)}, f32[400,6400]{1,0:T(8,128)}, u32[]{:S(2)}) copy-start(f32[400,6400]{1,0:T(8,128)} %get-tuple-element.139) | copy-start | bytes 30720004 | tf_op jit(solution)/shard_map/while
  289.4 4.4 %copy-start = (f32[400,6400]{1,0:T(8,128)S(1)}, f32[400,6400]{1,0:T(8,128)}, u32[]{:S(2)}) copy-start(f32[400,6400]{1,0:T(8,128)} %get-tuple-element.139) | copy-start | bytes 30720004 | tf_op jit(solution)/shard_map/while
  299.7 4.4 %copy-start = (f32[400,6400]{1,0:T(8,128)S(1)}, f32[400,6400]{1,0:T(8,128)}, u32[]{:S(2)}) copy-start(f32[400,6400]{1,0:T(8,128)} %get-tuple-element.139) | copy-start | bytes 30720004 | tf_op jit(solution)/shard_map/while
  309.9 4.4 %copy-start = (f32[400,6400]{1,0:T(8,128)S(1)}, f32[400,6400]{1,0:T(8,128)}, u32[]{:S(2)}) copy-start(f32[400,6400]{1,0:T(8,128)} %get-tuple-element.139) | copy-start | bytes 30720004 | tf_op jit(solution)/shard_map/while
  320.2 4.4 %copy-start = (f32[400,6400]{1,0:T(8,128)S(1)}, f32[400,6400]{1,0:T(8,128)}, u32[]{:S(2)}) copy-start(f32[400,6400]{1,0:T(8,128)} %get-tuple-element.139) | copy-start | bytes 30720004 | tf_op jit(solution)/shard_map/while
  330.4 4.4 %copy-start = (f32[400,6400]{1,0:T(8,128)S(1)}, f32[400,6400]{1,0:T(8,128)}, u32[]{:S(2)}) copy-start(f32[400,6400]{1,0:T(8,128)} %get-tuple-element.139) | copy-start | bytes 30720004 | tf_op jit(solution)/shard_map/while
Sparse Core Ops, SparseCore 0:
  10.1 99.6 all-gather.4
  111.4 106.1 all-gather.6
where the time goes:
time: 382 us; the launch traced here: 381 us
  matrix products  146 us (38%)
  waiting for transfers between devices  90.3 us (24%)
  blocking collectives  80.1 us (21%)
  local copies, waits for them, and re-layouts  37.2 us (10%)
  between operations  14.2 us (4%)
  other arithmetic  9.22 us (2%)
  starting transfers between devices  4.76 us (1%)
    dot_general x12, matrix products, per_walker(): forward = jnp.dot(left_orb, trial.T, preferred_element_type=jnp.float32)  61.2 us
    all_gather x1, waiting for transfers between devices, body(): lax.all_gather(orbit, 'pts', axis=0, tiled=True)  48.3 us
    dot_general x3, matrix products, body(): jnp.einsum('pi,pc->ic', map_full, scaled_cols, preferred_element_type=jnp...  40 us
    dot_general x12, matrix products, per_walker(): jnp.dot(trial_here, right_orb.T, preferred_element_type=jnp.float32)  37.1 us
    all_gather x1, waiting for transfers between devices, body(): map_full = lax.all_gather(points_map, 'pts', axis=0, tiled=True)  36.2 us
    psum x1, blocking collectives, body(): energy = lax.psum((hartree - exchange) / (2.0 * total_points), 'pts')  33.1 us
    all_gather x1, blocking collectives, body(): lax.all_gather(density, 'pts', axis=0, tiled=True)  25.9 us
    all_gather x1, blocking collectives, body(): field_full = lax.all_gather(field, 'pts', axis=0, tiled=True)  21.2 us
  transfers between devices with their start and end apart: 3, of which 3 were waited for; matrix products, arithmetic and copies ran while one was open for 18% of the time, Pallas kernels for 0%

commit v1 on v0

--- a/solution.py
+++ b/solution.py
@@ -60,8 +60,11 @@
     total_points = point_rows * lax.axis_size("pts")
     energy = lax.psum((hartree - exchange) / (2.0 * total_points), "pts")
     own_rows = orbitals // lax.axis_size("pts")
-    map_full = lax.all_gather(points_map, "pts", axis=0, tiled=True)
-    field_full = lax.all_gather(field, "pts", axis=0, tiled=True)
+    map_full, field_full = jnp.split(
+        lax.all_gather(jnp.concatenate([points_map, field], axis=1), "pts", axis=0, tiled=True),
+        [points_map.shape[1]],
+        axis=1,
+    )
     own_cols = walker_count * occupied // lax.axis_size("pts")
     col_start = lax.axis_index("pts") * own_cols
     cols_walkers = lax.dynamic_slice_in_dim(flat_walkers, col_start, own_cols, 1)

time: 382 us -> 440 us (1.15)
  waiting for transfers between devices: 90.3 us -> 138 us
  blocking collectives: 80.1 us -> 57 us
  matrix products: 146 us -> 166 us
  local copies, waits for them, and re-layouts: 37.2 us -> 48.4 us
    all_gather x1, waiting for transfers between devices: 36.2 us -> 103 us  [body(): lax.all_gather(jnp.concatenate([points_map, field], axis=1), 'pts', axis=...]
    all_gather x1 -> x0, blocking collectives: 21.2 us -> none  [body(): field_full = lax.all_gather(field, 'pts', axis=0, tiled=True)]
    dot_general x3, matrix products: 40 us -> 59.3 us  [body(): jnp.einsum('pi,pc->ic', map_full, scaled_cols, preferred_element_type=jnp...]
    all_gather x1, waiting for transfers between devices: 48.3 us -> 34.4 us  [body(): lax.all_gather(orbit, 'pts', axis=0, tiled=True)]
    all_to_all x1, waiting for transfers between devices: 5.06 us -> 0.01 us  [body(): lax.all_to_all(running_cols.astype(jnp.bfloat16), 'pts', split_axis=0, co...]
    split x0 -> x1, local copies, waits for them, and re-layouts: none -> 4.52 us  [body(): jnp.split(lax.all_gather(jnp.concatenate([points_map, field], axis=1), 'p...]
    unnamed x12 -> x8, local copies, waits for them, and re-layouts: 5.83 us -> 8.92 us
  transfers between devices with their start and end apart: 3 -> 3, of which waited for: 3 -> 2; matrix products, arithmetic and copies ran while one was open for 18% -> 43% of each run, Pallas kernels for 0% -> 0%
where the time goes in v1:
time: 440 us; the launch traced here: 439 us
  matrix products  166 us (38%)
  waiting for transfers between devices  138 us (31%)
  blocking collectives  57 us (13%)
  local copies, waits for them, and re-layouts  48.4 us (11%)
  between operations  14.2 us (3%)
  other arithmetic  11.2 us (3%)
  starting transfers between devices  4.97 us (1%)
    all_gather x1, waiting for transfers between devices, body(): lax.all_gather(jnp.concatenate([points_map, field], axis=1), 'pts', axis=...  103 us
    dot_general x12, matrix products, per_walker(): forward = jnp.dot(left_orb, trial.T, preferred_element_type=jnp.float32)  61.1 us
    dot_general x3, matrix products, body(): jnp.einsum('pi,pc->ic', map_full, scaled_cols, preferred_element_type=jnp...  59.3 us
    dot_general x12, matrix products, per_walker(): jnp.dot(trial_here, right_orb.T, preferred_element_type=jnp.float32)  37 us
    all_gather x1, waiting for transfers between devices, body(): lax.all_gather(orbit, 'pts', axis=0, tiled=True)  34.4 us
    psum x1, blocking collectives, body(): energy = lax.psum((hartree - exchange) / (2.0 * total_points), 'pts')  33.1 us
    all_gather x1, blocking collectives, body(): lax.all_gather(density, 'pts', axis=0, tiled=True)  23.8 us
    while x24, local copies, waits for them, and re-layouts  15.8 us
  transfers between devices with their start and end apart: 3, of which 2 were waited for; matrix products, arithmetic and copies ran while one was open for 43% of the time, Pallas kernels for 0%

profile of v1, /device:TPU:0, one launch (start us, length us, event | category | flops | bytes accessed | tf_op | source)
XLA Modules:
  0.0 439.2 jit_solution(7952146809019479113)
XLA Ops:
  7.2 4.5 %copy.19 = bf16[800,12,128]{0,2,1:T(8,128)(2,1)} copy(bf16[800,12,128]{2,0,1:T(8,128)(2,1)} %param.10) | data formatting | bytes 4915200 | tf_op args[3]
  20.7 23.8 %all-gather = bf16[16,400,12]{1,2,0:T(8,128)(2,1)S(1)} all-gather(bf16[1,400,12]{1,2,0:T(8,128)(2,1)S(1)} %fusion.116), channel_id=1, replica_groups=mesh['mol'=2,'pts'=16] {'pts'}, dimensions={0}, use_global_device_ids=true | all-gather | bytes 163200 | tf_op jit(solution)/shard_map/all_gather | solution.py:39
  54.8 7.9 %convert_element_type.95 = f32[400,6400]{1,0:T(8,128)} convert(bf16[400,6400]{1,0:T(8,128)(2,1)} %param.9) | non-fusion elementwise | flops 2560000 | bytes 15360000 | tf_op jit(solution)/shard_map/convert_element_type | solution.py:44
  64.2 103.3 %all-gather.4.cloned.1.call-done = f32[6400,812]{1,0:T(8,128)} async-done(((f32[400,812]{1,0:T(8,128)}), f32[6400,812]{1,0:T(8,128)}) %all-gather.4.cloned.1.call-update) | async-done | bytes 20787216 | tf_op jit(solution)/shard_map/all_gather | solution.py:64
  167.5 4.5 %split.9 = f32[6400,12]{1,0:T(8,128)} slice(f32[6400,812]{1,0:T(8,128)} %all-gather.4.cloned.1.call-done), slice={[0:6400], [800:812]} | slice | bytes 614400 | tf_op jit(solution)/shard_map/split | solution.py:63
  175.9 19.8 %fusion.109 = bf16[800,96]{0,1:T(8,128)(2,1)S(1)} fusion(f32[6400,812]{1,0:T(8,128)} %all-gather.4.cloned.1.call-done, f32[96,6400]{1,0:T(8,128)S(1)} %gather_fusion, pred[96]{0:T(512)(128)(4,1)S(1)} %compare_and_fusion, bf16[800,1536]{0,1:T(8,128)(2,1)} %bitcast.77, s32[]{:T(128)S(6)} %select_n.54), kind=kOutput, calls=%fused_computation.58 | convolution fusion | flops 1968537600 | bytes 25720932 | tf_op jit(solution)/shard_map/pi,pc->ic/dot_general | solution.py:80
  195.7 19.7 %fusion.104 = bf16[800,96]{0,1:T(8,128)(2,1)S(1)} fusion(bf16[800,96]{0,1:T(8,128)(2,1)S(1)} %fusion.109, f32[6400,812]{1,0:T(8,128)} %all-gather.4.cloned.1.call-done, f32[96,6400]{1,0:T(8,128)S(1)} %gather_fusion, pred[96]{0:T(512)(128)(4,1)S(1)} %compare_and_fusion), kind=kOutput, calls=%fused_computation.57 | convolution fusion | flops 1968691200 | bytes 23552096 | tf_op jit(solution)/shard_map/pi,pc->ic/dot_general | solution.py:80
  215.4 19.9 %fusion.99 = bf16[800,96]{0,1:T(8,128)(2,1)S(1)} fusion(bf16[800,96]{0,1:T(8,128)(2,1)S(1)} %fusion.104, f32[6400,812]{1,0:T(8,128)} %all-gather.4.cloned.1.call-done, f32[96,6400]{1,0:T(8,128)S(1)} %gather_fusion, pred[96]{0:T(512)(128)(4,1)S(1)} %compare_and_fusion, bf16[800,96]{0,1:T(8,128)(2,1)S(1)} %fusion.109, bf16[800,1536]{0,1:T(8,128)(2,1)} %bitcast.78, ...), kind=kOutput, calls=%fused_computation.56 | convolution fusion | flops 1969305600 | bytes 24068612 | tf_op jit(solution)/shard_map/pi,pc->ic/dot_general | solution.py:80
  236.3 4.7 %all-to-all-start = ((bf16[16,50,96]{2,1,0:T(8,128)(2,1)}), bf16[16,50,96]{2,1,0:T(8,128)(2,1)S(1)}, u32[]{:S(2)}, u32[]{:S(2)}) async-start(bf16[16,50,96]{2,1,0:T(8,128)(2,1)} %all_to_all.12), calls=%async_computation | async-start | bytes 458752 | tf_op jit(solution)/shard_map/all_to_all | solution.py:85
  241.0 34.4 %all-gather.6.cloned.1.call-done = bf16[6400,12,128]{2,0,1:T(8,128)(2,1)} async-done(((bf16[400,12,128]{2,0,1:T(8,128)(2,1)}), bf16[6400,12,128]{2,0,1:T(8,128)(2,1)}) %all-gather.6.cloned.1.call-update) | async-done | bytes 19660816 | tf_op jit(solution)/shard_map/all_gather | solution.py:55
  275.4 123.0 %while.10 = (s32[]{:T(128)}, f32[12]{0:T(128)S(1)}, bf16[12,400,128]{2,1,0:T(8,128)(2,1)}, bf16[6400,128]{1,0:T(8,128)(2,1)}, f32[400,6400]{1,0:T(8,128)}, /*ind...) while((s32[]{:T(128)}, f32[12]{0:T(128)S(1)}, bf16[12,400,128]{2,1,0:T(8,128)(2,1)}, ...), condition=%wide.region_4.5_spmd, body=%wide.region_2.4_spmd.sunk | while | flops 1318400000 | bytes 75162760 | solution.py:53
  279.8 5.1 %fusion.142 = f32[]{:T(128)} fusion(f32[400,6400]{1,0:T(8,128)S(1)} %convolution_bitcast_fusion.3, f32[400,6400]{1,0:T(8,128)S(1)} %copy-done, bf16[6400,128]{1,0:T(8,128)(2,1)} %get-tuple-element.138, bf16[12,400,128]{2,1,0:T(8,128)(2,1)} %get-tuple-element.137, s32[]{:T(128)} %get-tuple-element.127), kind=kOutput, calls=%fused_computation.4.clone.1 | convolution fusion | flops 663040000 | bytes 22221316 | tf_op jit(solution)/shard_map/while/body/eval_jaxpr/dot_general | solution.py:48
  290.0 5.1 %fusion.142 = f32[]{:T(128)} fusion(f32[400,6400]{1,0:T(8,128)S(1)} %convolution_bitcast_fusion.3, f32[400,6400]{1,0:T(8,128)S(1)} %copy-done, bf16[6400,128]{1,0:T(8,128)(2,1)} %get-tuple-element.138, bf16[12,400,128]{2,1,0:T(8,128)(2,1)} %get-tuple-element.137, s32[]{:T(128)} %get-tuple-element.127), kind=kOutput, calls=%fused_computation.4.clone.1 | convolution fusion | flops 663040000 | bytes 22221316 | tf_op jit(solution)/shard_map/while/body/eval_jaxpr/dot_general | solution.py:48
  300.3 5.1 %fusion.142 = f32[]{:T(128)} fusion(f32[400,6400]{1,0:T(8,128)S(1)} %convolution_bitcast_fusion.3, f32[400,6400]{1,0:T(8,128)S(1)} %copy-done, bf16[6400,128]{1,0:T(8,128)(2,1)} %get-tuple-element.138, bf16[12,400,128]{2,1,0:T(8,128)(2,1)} %get-tuple-element.137, s32[]{:T(128)} %get-tuple-element.127), kind=kOutput, calls=%fused_computation.4.clone.1 | convolution fusion | flops 663040000 | bytes 22221316 | tf_op jit(solution)/shard_map/while/body/eval_jaxpr/dot_general | solution.py:48
  310.5 5.1 %fusion.142 = f32[]{:T(128)} fusion(f32[400,6400]{1,0:T(8,128)S(1)} %convolution_bitcast_fusion.3, f32[400,6400]{1,0:T(8,128)S(1)} %copy-done, bf16[6400,128]{1,0:T(8,128)(2,1)} %get-tuple-element.138, bf16[12,400,128]{2,1,0:T(8,128)(2,1)} %get-tuple-element.137, s32[]{:T(128)} %get-tuple-element.127), kind=kOutput, calls=%fused_computation.4.clone.1 | convolution fusion | flops 663040000 | bytes 22221316 | tf_op jit(solution)/shard_map/while/body/eval_jaxpr/dot_general | solution.py:48
  320.8 5.1 %fusion.142 = f32[]{:T(128)} fusion(f32[400,6400]{1,0:T(8,128)S(1)} %convolution_bitcast_fusion.3, f32[400,6400]{1,0:T(8,128)S(1)} %copy-done, bf16[6400,128]{1,0:T(8,128)(2,1)} %get-tuple-element.138, bf16[12,400,128]{2,1,0:T(8,128)(2,1)} %get-tuple-element.137, s32[]{:T(128)} %get-tuple-element.127), kind=kOutput, calls=%fused_computation.4.clone.1 | convolution fusion | flops 663040000 | bytes 22221316 | tf_op jit(solution)/shard_map/while/body/eval_jaxpr/dot_general | solution.py:48
  331.0 5.1 %fusion.142 = f32[]{:T(128)} fusion(f32[400,6400]{1,0:T(8,128)S(1)} %convolution_bitcast_fusion.3, f32[400,6400]{1,0:T(8,128)S(1)} %copy-done, bf16[6400,128]{1,0:T(8,128)(2,1)} %get-tuple-element.138, bf16[12,400,128]{2,1,0:T(8,128)(2,1)} %get-tuple-element.137, s32[]{:T(128)} %get-tuple-element.127), kind=kOutput, calls=%fused_computation.4.clone.1 | convolution fusion | flops 663040000 | bytes 22221316 | tf_op jit(solution)/shard_map/while/body/eval_jaxpr/dot_general | solution.py:48
  341.2 5.1 %fusion.142 = f32[]{:T(128)} fusion(f32[400,6400]{1,0:T(8,128)S(1)} %convolution_bitcast_fusion.3, f32[400,6400]{1,0:T(8,128)S(1)} %copy-done, bf16[6400,128]{1,0:T(8,128)(2,1)} %get-tuple-element.138, bf16[12,400,128]{2,1,0:T(8,128)(2,1)} %get-tuple-element.137, s32[]{:T(128)} %get-tuple-element.127), kind=kOutput, calls=%fused_computation.4.clone.1 | convolution fusion | flops 663040000 | bytes 22221316 | tf_op jit(solution)/shard_map/while/body/eval_jaxpr/dot_general | solution.py:48
  351.5 5.1 %fusion.142 = f32[]{:T(128)} fusion(f32[400,6400]{1,0:T(8,128)S(1)} %convolution_bitcast_fusion.3, f32[400,6400]{1,0:T(8,128)S(1)} %copy-done, bf16[6400,128]{1,0:T(8,128)(2,1)} %get-tuple-element.138, bf16[12,400,128]{2,1,0:T(8,128)(2,1)} %get-tuple-element.137, s32[]{:T(128)} %get-tuple-element.127), kind=kOutput, calls=%fused_computation.4.clone.1 | convolution fusion | flops 663040000 | bytes 22221316 | tf_op jit(solution)/shard_map/while/body/eval_jaxpr/dot_general | solution.py:48
  361.7 5.1 %fusion.142 = f32[]{:T(128)} fusion(f32[400,6400]{1,0:T(8,128)S(1)} %convolution_bitcast_fusion.3, f32[400,6400]{1,0:T(8,128)S(1)} %copy-done, bf16[6400,128]{1,0:T(8,128)(2,1)} %get-tuple-element.138, bf16[12,400,128]{2,1,0:T(8,128)(2,1)} %get-tuple-element.137, s32[]{:T(128)} %get-tuple-element.127), kind=kOutput, calls=%fused_computation.4.clone.1 | convolution fusion | flops 663040000 | bytes 22221316 | tf_op jit(solution)/shard_map/while/body/eval_jaxpr/dot_general | solution.py:48
  372.0 5.1 %fusion.142 = f32[]{:T(128)} fusion(f32[400,6400]{1,0:T(8,128)S(1)} %convolution_bitcast_fusion.3, f32[400,6400]{1,0:T(8,128)S(1)} %copy-done, bf16[6400,128]{1,0:T(8,128)(2,1)} %get-tuple-element.138, bf16[12,400,128]{2,1,0:T(8,128)(2,1)} %get-tuple-element.137, s32[]{:T(128)} %get-tuple-element.127), kind=kOutput, calls=%fused_computation.4.clone.1 | convolution fusion | flops 663040000 | bytes 22221316 | tf_op jit(solution)/shard_map/while/body/eval_jaxpr/dot_general | solution.py:48
  382.2 5.1 %fusion.142 = f32[]{:T(128)} fusion(f32[400,6400]{1,0:T(8,128)S(1)} %convolution_bitcast_fusion.3, f32[400,6400]{1,0:T(8,128)S(1)} %copy-done, bf16[6400,128]{1,0:T(8,128)(2,1)} %get-tuple-element.138, bf16[12,400,128]{2,1,0:T(8,128)(2,1)} %get-tuple-element.137, s32[]{:T(128)} %get-tuple-element.127), kind=kOutput, calls=%fused_computation.4.clone.1 | convolution fusion | flops 663040000 | bytes 22221316 | tf_op jit(solution)/shard_map/while/body/eval_jaxpr/dot_general | solution.py:48
  392.5 5.1 %fusion.142 = f32[]{:T(128)} fusion(f32[400,6400]{1,0:T(8,128)S(1)} %convolution_bitcast_fusion.3, f32[400,6400]{1,0:T(8,128)S(1)} %copy-done, bf16[6400,128]{1,0:T(8,128)(2,1)} %get-tuple-element.138, bf16[12,400,128]{2,1,0:T(8,128)(2,1)} %get-tuple-element.137, s32[]{:T(128)} %get-tuple-element.127), kind=kOutput, calls=%fused_computation.4.clone.1 | convolution fusion | flops 663040000 | bytes 22221316 | tf_op jit(solution)/shard_map/while/body/eval_jaxpr/dot_general | solution.py:48
  398.3 33.1 %psum.7 = f32[12]{0:T(128)} all-reduce(f32[12]{0:T(128)S(1)} %subtract_multiply_fusion.1), channel_id=1, replica_groups=mesh['mol'=2,'pts'=16] {'pts'}, use_global_device_ids=true, to_apply=%region_5.6 | all-reduce | flops 12 | bytes 96 | tf_op jit(solution)/shard_map/psum | solution.py:61
  (83 shorter events, 88.3 us)
Async XLA Ops:
  7.2 160.3 %all-gather.4.cloned.1.call-start = ((), (), s32[]{:S(2)}) async-start(), calls=%async_computation.1 | async-start | bytes 24371200 | tf_op jit(solution)/shard_map/all_gather | solution.py:64
  7.2 4.5 %copy-start.1 = (bf16[400,800]{1,0:T(8,128)(2,1)S(1)}, bf16[400,800]{1,0:T(8,128)(2,1)}, u32[]{:S(2)}) copy-start(bf16[400,800]{1,0:T(8,128)(2,1)} %param.7) | copy-start | bytes 1920004
  18.7 27.9 %copy-start.2 = (s32[400,12]{0,1:T(8,128)S(1)}, s32[400,12]{0,1:T(8,128)}, u32[]{:S(2)}) copy-start(s32[400,12]{0,1:T(8,128)} %param.11) | copy-start | bytes 57604
  52.1 223.3 %all-gather.6.cloned.1.call-start = ((), (), s32[]{:S(2)}) async-start(), calls=%async_computation.2 | async-start | bytes 20889600 | tf_op jit(solution)/shard_map/all_gather | solution.py:55
  236.3 195.2 %all-to-all-start = ((bf16[16,50,96]{2,1,0:T(8,128)(2,1)}), bf16[16,50,96]{2,1,0:T(8,128)(2,1)S(1)}, u32[]{:S(2)}, u32[]{:S(2)}) async-start(bf16[16,50,96]{2,1,0:T(8,128)(2,1)} %all_to_all.12), calls=%async_computation | async-start | bytes 458752 | tf_op jit(solution)/shard_map/all_to_all | solution.py:85
  275.4 4.4 %copy-start = (f32[400,6400]{1,0:T(8,128)S(1)}, f32[400,6400]{1,0:T(8,128)}, u32[]{:S(2)}) copy-start(f32[400,6400]{1,0:T(8,128)} %get-tuple-element.139) | copy-start | bytes 30720004 | tf_op jit(solution)/shard_map/while
  285.6 4.4 %copy-start = (f32[400,6400]{1,0:T(8,128)S(1)}, f32[400,6400]{1,0:T(8,128)}, u32[]{:S(2)}) copy-start(f32[400,6400]{1,0:T(8,128)} %get-tuple-element.139) | copy-start | bytes 30720004 | tf_op jit(solution)/shard_map/while
  295.9 4.4 %copy-start = (f32[400,6400]{1,0:T(8,128)S(1)}, f32[400,6400]{1,0:T(8,128)}, u32[]{:S(2)}) copy-start(f32[400,6400]{1,0:T(8,128)} %get-tuple-element.139) | copy-start | bytes 30720004 | tf_op jit(solution)/shard_map/while
  306.1 4.4 %copy-start = (f32[400,6400]{1,0:T(8,128)S(1)}, f32[400,6400]{1,0:T(8,128)}, u32[]{:S(2)}) copy-start(f32[400,6400]{1,0:T(8,128)} %get-tuple-element.139) | copy-start | bytes 30720004 | tf_op jit(solution)/shard_map/while
  316.3 4.4 %copy-start = (f32[400,6400]{1,0:T(8,128)S(1)}, f32[400,6400]{1,0:T(8,128)}, u32[]{:S(2)}) copy-start(f32[400,6400]{1,0:T(8,128)} %get-tuple-element.139) | copy-start | bytes 30720004 | tf_op jit(solution)/shard_map/while
  326.6 4.4 %copy-start = (f32[400,6400]{1,0:T(8,128)S(1)}, f32[400,6400]{1,0:T(8,128)}, u32[]{:S(2)}) copy-start(f32[400,6400]{1,0:T(8,128)} %get-tuple-element.139) | copy-start | bytes 30720004 | tf_op jit(solution)/shard_map/while
  336.8 4.4 %copy-start = (f32[400,6400]{1,0:T(8,128)S(1)}, f32[400,6400]{1,0:T(8,128)}, u32[]{:S(2)}) copy-start(f32[400,6400]{1,0:T(8,128)} %get-tuple-element.139) | copy-start | bytes 30720004 | tf_op jit(solution)/shard_map/while
  347.1 4.4 %copy-start = (f32[400,6400]{1,0:T(8,128)S(1)}, f32[400,6400]{1,0:T(8,128)}, u32[]{:S(2)}) copy-start(f32[400,6400]{1,0:T(8,128)} %get-tuple-element.139) | copy-start | bytes 30720004 | tf_op jit(solution)/shard_map/while
  357.3 4.4 %copy-start = (f32[400,6400]{1,0:T(8,128)S(1)}, f32[400,6400]{1,0:T(8,128)}, u32[]{:S(2)}) copy-start(f32[400,6400]{1,0:T(8,128)} %get-tuple-element.139) | copy-start | bytes 30720004 | tf_op jit(solution)/shard_map/while
  367.6 4.4 %copy-start = (f32[400,6400]{1,0:T(8,128)S(1)}, f32[400,6400]{1,0:T(8,128)}, u32[]{:S(2)}) copy-start(f32[400,6400]{1,0:T(8,128)} %get-tuple-element.139) | copy-start | bytes 30720004 | tf_op jit(solution)/shard_map/while
  377.8 4.4 %copy-start = (f32[400,6400]{1,0:T(8,128)S(1)}, f32[400,6400]{1,0:T(8,128)}, u32[]{:S(2)}) copy-start(f32[400,6400]{1,0:T(8,128)} %get-tuple-element.139) | copy-start | bytes 30720004 | tf_op jit(solution)/shard_map/while
  388.1 4.4 %copy-start = (f32[400,6400]{1,0:T(8,128)S(1)}, f32[400,6400]{1,0:T(8,128)}, u32[]{:S(2)}) copy-start(f32[400,6400]{1,0:T(8,128)} %get-tuple-element.139) | copy-start | bytes 30720004 | tf_op jit(solution)/shard_map/while
Sparse Core Ops, SparseCore 0:
  52.2 115.2 all-gather.3
  169.0 106.2 all-gather.5
